TPU v7x, 32 devices: a whole 2x2x4 slice. The times are simulated.
32 devices in a mesh: rep: 8 (over y, x, core), tp: 4 (over z).
Axes of the slice: x: 2, y: 2, z: 4, core: 2. Of those that a mesh axis runs over, the one named last changes fastest.
Arguments:
- residual_in: bfloat16 [8, 512, 8192], P('rep', 'tp'), may hold values from -6 to 6
- norm_gain: bfloat16 [8192], replicated, may hold values from 0.099609375 to 1.8984375
- w_query: bfloat16 [8192, 4096], P(None, 'tp'), may hold values from -1 to 1
- w_keyval: bfloat16 [8192, 1024], P(None, 'tp'), may hold values from -0.0625 to 0.0625
- w_out: bfloat16 [4096, 8192], P('tp'), may hold values from -0.375 to 0.375
- score_head: bfloat16 [8192], replicated, may hold values from -0.0625 to 0.0625
- lengths: int32 [8], P('rep'), may hold values from 256 to 512
- policy_slots: bfloat16 [8, 768, 8192], P('rep', None, 'tp'), may hold values from -6 to 6
Outputs:
- scored_hidden: bfloat16 [8, 512, 8192], P('rep', 'tp')
- rewards: float32 [8], P('rep')
- policy_copies: bfloat16 [8, 768, 8192], P('rep', None, 'tp')
All inputs are finite; a program needn't handle non-finite values.
Results may differ from a plain program's by a relative error of at most 0.017.
The roundings to bfloat16 on the way count: a program that leaves them out, or rounds other values in their place, can miss the bound.
Values may be sent and summed in bfloat16 or wider, within the bound.
A program may use at most 128 MiB of HBM per device.

v0:
```python
import jax
import jax.numpy as jnp
from jax import lax
from jax.sharding import PartitionSpec as P

QH = 32
KVH = 4
HS = 128
KW = 512


def from_root(value, axis, source):
    kept = jnp.where(lax.axis_index(axis) == source, value, 0).astype(value.dtype)
    return lax.psum(kept, axis)


def on_device(residual_in, norm_gain, w_query, w_keyval, w_out, score_head, lengths, policy_slots):
    tp_index = lax.axis_index("tp")
    local_rows = residual_in.shape[1]
    resid = residual_in[0].astype(jnp.float32)
    meansq = jnp.mean(resid * resid, axis=-1, keepdims=True)
    normed = (resid * lax.rsqrt(meansq + 1e-05) * norm_gain.astype(jnp.float32)).astype(
        jnp.bfloat16
    )
    query_cols = w_query.shape[1]
    piece = lax.all_gather(normed, "tp", axis=0, tiled=True)
    query_part = jnp.dot(piece, w_query, preferred_element_type=jnp.float32).astype(jnp.bfloat16)
    pair_part = jnp.dot(piece, w_keyval, preferred_element_type=jnp.float32).astype(jnp.bfloat16)
    projected = jnp.concatenate([query_part, pair_part], axis=1)
    queries = projected[:, :query_cols]
    keyval_local = projected[:, query_cols:]
    keyval_full = lax.all_gather(keyval_local, "tp", axis=1, tiled=True)
    seq_total = keyval_full.shape[0]
    heads_here = query_cols // HS
    group = QH // KVH
    rowpos = jnp.arange(seq_total, dtype=jnp.int32)[:, None]
    colpos = jnp.arange(seq_total, dtype=jnp.int32)[None, :]
    length = lengths[0]
    valid = (colpos <= rowpos) & (colpos < length)
    outputs = []
    for local_head in range(heads_here):
        head_id = tp_index * heads_here + local_head
        kv_head = head_id // group
        keys = lax.dynamic_slice_in_dim(keyval_full, kv_head * HS, HS, 1)
        values = lax.dynamic_slice_in_dim(keyval_full, KW + kv_head * HS, HS, 1)
        query_head = queries[:, local_head * HS : (local_head + 1) * HS]
        scores = lax.dot_general(
            query_head, keys, (((1,), (1,)), ((), ())), preferred_element_type=jnp.float32
        ) * HS ** (-0.5)
        scores = jnp.where(valid, scores, -1e30)
        probs = jax.nn.softmax(scores, axis=-1).astype(jnp.bfloat16)
        outputs.append(
            jnp.dot(probs, values, preferred_element_type=jnp.float32).astype(jnp.bfloat16)
        )
    attended = jnp.concatenate(outputs, axis=1)
    summed = lax.psum_scatter(
        jnp.dot(attended, w_out, preferred_element_type=jnp.float32).astype(jnp.bfloat16),
        "tp",
        scatter_dimension=0,
        tiled=True,
    ).astype(jnp.float32)
    hidden = (resid + summed).astype(jnp.bfloat16)
    local_last = length - 1 - tp_index * local_rows
    picker = (jnp.arange(local_rows, dtype=jnp.int32) == local_last).astype(jnp.float32)
    weights = picker + seq_total ** (-0.5)
    row_scores = jnp.sum(
        hidden.astype(jnp.float32) * score_head.astype(jnp.float32)[None, :], axis=1
    )
    contrib = jnp.sum(row_scores * weights)
    reward = lax.psum(contrib, "tp")
    policy_copy = from_root(policy_slots, "rep", 0)
    return (hidden[None], reward.reshape(1), policy_copy)


def solution(mesh):
    placed = (
        P("rep", "tp", None),
        P(),
        P(None, "tp"),
        P(None, "tp"),
        P("tp", None),
        P(),
        P("rep"),
        P("rep", None, "tp"),
    )
    return jax.shard_map(
        on_device,
        mesh=mesh,
        in_specs=placed,
        out_specs=(P("rep", "tp", None), P("rep"), P("rep", None, "tp")),
        check_vma=False,
    )
```

profile of v0, /device:TPU:0, one launch (start us, length us, event | category | flops | bytes accessed | tf_op | source)
XLA Modules:
  0.0 396.8 jit_solution(10901938916231230851)
XLA Ops:
  8.0 0.0 all-gather.3.cloned.1.call-start
  8.0 0.7 convert_element_type.88
  8.8 2.1 fusion
  10.9 3.5 fusion.2
  14.4 0.0 all-gather.3.cloned.1.call-update
  14.4 0.0 all-gather.5.cloned.1.call-start
  15.2 151.7 %all-gather.3.cloned.1.call-done = bf16[512,8192]{1,0:T(8,128)(2,1)} async-done(((bf16[128,8192]{1,0:T(8,128)(2,1)}), bf16[512,8192]{1,0:T(8,128)(2,1)}) %all-gather.3.cloned.1.call-update) | async-done | bytes 8388624 | tf_op jit(solution)/shard_map/all_gather | solution.py:26
  166.9 7.6 %convolution_convert_fusion.2 = bf16[512,256]{1,0:T(8,128)(2,1)} fusion(bf16[512,8192]{1,0:T(8,128)(2,1)} %all-gather.3.cloned.1.call-done, bf16[8192,256]{1,0:T(8,128)(2,1)} %param.11), kind=kOutput, calls=%fused_computation.27 | convolution fusion | flops 2147614720 | bytes 12845056 | tf_op jit(solution)/shard_map/dot_general | solution.py:28
  174.5 0.0 all-gather.5.cloned.1.call-update
  174.5 0.2 reduce-scatter.2.cloned.1.call-start
  174.7 14.9 %convolution_convert_fusion.1 = bf16[512,1024]{1,0:T(8,128)(2,1)S(1)} fusion(bf16[512,8192]{1,0:T(8,128)(2,1)} %all-gather.3.cloned.1.call-done, bf16[8192,1024]{1,0:T(8,128)(2,1)} %param.10), kind=kOutput, calls=%fused_computation.10 | convolution fusion | flops 8590458880 | bytes 26214400 | tf_op jit(solution)/shard_map/dot_general | solution.py:27
  189.7 13.1 %all-gather.5.cloned.1.call-done = bf16[512,1024]{1,0:T(8,128)(2,1)} async-done(((bf16[512,256]{1,0:T(8,128)(2,1)}), bf16[512,1024]{1,0:T(8,128)(2,1)}) %all-gather.5.cloned.1.call-update) | async-done | bytes 1048592 | tf_op jit(solution)/shard_map/all_gather | solution.py:32
  202.8 0.0 copy-start.2
  202.8 1.3 fusion.93
  204.1 0.2 fusion.25
  204.3 1.2 fusion.92
  205.5 0.2 fusion.24
  205.7 0.0 copy-done.2
  205.7 0.3 fusion.91
  206.1 0.2 fusion.23
  206.3 0.3 fusion.90
  206.6 0.2 fusion.22
  206.8 0.3 fusion.89
  207.2 0.2 fusion.21
  207.4 0.3 fusion.94
  207.7 0.2 fusion.26
  207.9 0.4 fusion.95
  208.3 0.2 fusion.27
  208.5 0.3 fusion.96
  208.8 0.2 fusion.28
  209.0 0.4 fusion.19
  209.4 0.0 slice-start
  209.4 0.4 fusion.18
  209.9 0.0 slice-start.1
  209.9 0.4 fusion.17
  210.3 0.4 fusion.16
  210.8 0.0 slice-start.2
  210.8 0.4 fusion.15
  211.2 0.4 fusion.14
  211.7 0.0 slice-start.3
  211.7 0.4 fusion.13
  212.1 0.5 fusion.12
  212.6 0.0 slice-done
  212.6 0.4 slice-done.1
  213.0 1.3 slice-done.2
  214.3 1.2 slice-done.3
  215.5 11.1 %convolution_convert_fusion = bf16[512,8192]{1,0:T(8,128)(2,1)} fusion(bf16[512,1024]{1,0:T(8,128)(2,1)S(1)} %fusion.12, bf16[1024,8192]{1,0:T(8,128)(2,1)S(1)} %bitcast.22), kind=kOutput, calls=%fused_computation | convolution fusion | flops 8594128896 | bytes 26214400 | tf_op jit(solution)/shard_map/dot_general | solution.py:57
  226.6 0.0 reduce-scatter.2.cloned.1.call-update
  226.7 0.0 all-reduce.2.cloned.1.call-start
  226.7 0.0 copy-start.1
  226.7 0.0 copy-start
  226.7 3.9 broadcast_select_fusion
  230.7 0.0 all-reduce.2.cloned.1.call-update
  230.7 0.0 copy-done.1
  230.7 139.0 %reduce-scatter.2.cloned.1.call-done = bf16[128,8192]{1,0:T(8,128)(2,1)} async-done(((bf16[512,8192]{1,0:T(8,128)(2,1)}), bf16[128,8192]{1,0:T(8,128)(2,1)}) %reduce-scatter.2.cloned.1.call-update) | async-done | bytes 2097168 | tf_op jit(solution)/shard_map/reduce_scatter | solution.py:56
  369.7 0.0 copy-done
  369.7 3.6 multiply_reduce_fusion
  373.4 0.6 fusion.88
  374.0 11.7 %psum.14 = f32[1]{0:T(128)} all-reduce(f32[1]{0:T(128)} %bitcast.4), channel_id=1, replica_groups=mesh['rep'=8,'tp'=4] {'tp'}, use_global_device_ids=true, to_apply=%region_20.21 | all-reduce | flops 1 | bytes 8 | tf_op jit(solution)/shard_map/psum | solution.py:70
  385.7 0.0 all-reduce.2.cloned.1.call-done
  385.7 4.0 %copy.20 = bf16[1,768,2048]{2,1,0:T(8,128)(2,1)} copy(bf16[1,768,2048]{2,1,0:T(8,128)(2,1)} %all-reduce.2.cloned.1.call-done) | data formatting | bytes 6291456
  (4 shorter events, 0.0 us)
Async XLA Ops:
  8.0 158.9 %all-gather.3.cloned.1.call-start = ((), (), s32[]{:S(2)}) async-start(), calls=%async_computation.1 | async-start | bytes 10485760 | tf_op jit(solution)/shard_map/all_gather | solution.py:26
  14.4 188.4 %all-gather.5.cloned.1.call-start = ((), (), s32[]{:S(2)}) async-start(), calls=%async_computation.2 | async-start | bytes 1310720 | tf_op jit(solution)/shard_map/all_gather | solution.py:32
  174.5 195.2 %reduce-scatter.2.cloned.1.call-start = ((), (), s32[]{:S(2)}) async-start(), calls=%async_computation.3 | async-start | bytes 10485760 | tf_op jit(solution)/shard_map/reduce_scatter | solution.py:56
  202.8 3.0 copy-start.2
  209.4 3.2 slice-start
  209.9 3.1 slice-start.1
  210.8 3.5 slice-start.2
  211.7 3.8 slice-start.3
  226.7 159.0 %all-reduce.2.cloned.1.call-start = ((), (), s32[]{:S(2)}) async-start(), calls=%async_computation.4 | async-start | bytes 6291456 | tf_op jit(solution)/shard_map/psum | solution.py:14
  226.7 4.0 %copy-start.1 = (bf16[8192]{0:T(1024)(128)(2,1)S(1)}, bf16[8192]{0:T(1024)(128)(2,1)}, u32[]{:S(2)}) copy-start(bf16[8192]{0:T(1024)(128)(2,1)} %param.13) | copy-start | bytes 49156
  226.7 143.0 %copy-start = (bf16[1,128,8192]{2,1,0:T(8,128)(2,1)S(1)}, bf16[1,128,8192]{2,1,0:T(8,128)(2,1)}, u32[]{:S(2)}) copy-start(bf16[1,128,8192]{2,1,0:T(8,128)(2,1)} %param.8) | copy-start | bytes 6291460
Sparse Core Ops, SparseCore 0:
  14.5 152.3 all-gather.2
  174.6 28.1 all-gather.4
  226.8 142.8 reduce-scatter.1
Sparse Core Ops, SparseCore 1:
  231.0 67.3 all-reduce.1
where the time goes:
time: 397 us
  waiting for transfers between devices  304 us (77%)
  matrix products  41.8 us (11%)
  other arithmetic  16.1 us (4%)
  between operations  16.1 us (4%)
  blocking collectives  11.7 us (3%)
  local copies, waits for them, and re-layouts  6.87 us (2%)
    all_gather x1, waiting for transfers between devices, on_device(): piece = lax.all_gather(normed, 'tp', axis=0, tiled=True)  152 us
    reduce_scatter x1, waiting for transfers between devices, on_device(): lax.psum_scatter(jnp.dot(attended, w_out, preferred_element_type=jnp.floa...  139 us
    dot_general x1, matrix products, on_device(): jnp.dot(piece, w_query, preferred_element_type=jnp.float32)  14.9 us
    all_gather x1, waiting for transfers between devices, on_device(): keyval_full = lax.all_gather(keyval_local, 'tp', axis=1, tiled=True)  13.1 us
    psum x1, blocking collectives, on_device(): reward = lax.psum(contrib, 'tp')  11.7 us
    dot_general x1, matrix products, on_device(): jnp.dot(attended, w_out, preferred_element_type=jnp.float32)  11.1 us
  transfers between devices with their start and end apart: 4, of which 3 were waited for; matrix products, arithmetic and copies ran while one was open for 6% of the time, Pallas kernels for 0%

commit v1 on v0

v1 whole, which is shorter than its diff:
```python
import functools

import jax
import jax.numpy as jnp
from jax import lax
from jax.experimental import pallas as pl
from jax.experimental.pallas import tpu as pltpu
from jax.sharding import PartitionSpec as P

QH = 32
KVH = 4
HS = 128
MESH = pl.DeviceIdType.MESH
F32 = jnp.float32
BF16 = jnp.bfloat16
CHUNKS = 16
LAG = 2


def kernel(
    n, R, kvw, heads,
    resid_h, gain, wq_h, wkv_h, wo_h, head, lens, pol_in,
    out_h, rew, pol_out,
    wq, wkv, wo, resid, nrm, part, qs, accq, acckv, kvown, kvin, kf, vf, att, rmy, rin,
    load_sem, ag_send, ag_recv, rs_send, rs_recv, kv_send, kv_recv, r_send, r_recv, p_send, p_recv, p_loc, out_sem,
):
    t = lax.axis_index("tp")
    r = lax.axis_index("rep")
    C = nrm.shape[1]
    rows, cols = nrm.shape[2], nrm.shape[3]
    seq = n * rows
    length = lens[0]

    def chunk_of(ref, c):
        return ref.at[:, pl.ds(pl.multiple_of(c * cols, cols), cols)]

    loads = [pltpu.make_async_copy(chunk_of(resid_h.at[0], c), resid.at[c], load_sem.at[c]) for c in range(C)]
    wloads = [
        pltpu.make_async_copy(wq_h, wq, load_sem.at[C]),
        pltpu.make_async_copy(wkv_h, wkv, load_sem.at[C + 1]),
    ]
    oloads = [pltpu.make_async_copy(chunk_of(wo_h, c), wo.at[c], load_sem.at[C + 2 + c]) for c in range(C)]
    for cp in loads + wloads + oloads:
        cp.start()
    kf[...] = jnp.zeros_like(kf)
    vf[...] = jnp.zeros_like(vf)

    barrier = pltpu.get_barrier_semaphore()
    for k in range(1, n):
        pl.semaphore_signal(barrier, inc=1, device_id={"tp": lax.rem(t + k, n)}, device_id_type=MESH)
    for k in range(1, R):
        pl.semaphore_signal(barrier, inc=1, device_id={"rep": lax.rem(r + k, R)}, device_id_type=MESH)

    for cp in loads:
        cp.wait()

    def sq(c, acc):
        x = resid[c].astype(F32)
        return acc + jnp.sum(x * x, axis=1, keepdims=True)

    ms = lax.fori_loop(0, C, sq, jnp.zeros((rows, 1), F32))
    scale = lax.rsqrt(ms / (C * cols) + 1e-05)

    def norm(c, carry):
        nrm[t, c] = (resid[c].astype(F32) * scale * gain[c].astype(F32)).astype(BF16)
        return carry

    lax.fori_loop(0, C, norm, 0)
    pl.semaphore_wait(barrier, n - 1 + R - 1)

    steps = R.bit_length() - 1

    def pol(src, s):
        return pltpu.make_async_remote_copy(
            src, pol_out, p_send.at[s], p_recv, device_id={"rep": r + (R >> (s + 1))}, device_id_type=MESH
        )

    @pl.when(r == 0)
    def _():
        for s in range(steps):
            pol(pol_in, s).start()
        pltpu.make_async_copy(pol_in, pol_out, p_loc).start()

    def pol_point(s):
        gap = R >> (s + 1)

        @pl.when(lax.rem(r, 2 * gap) == gap)
        def _():
            pltpu.make_async_copy(pol_out, pol_out, p_recv).wait()
            for q in range(s + 1, steps):
                pol(pol_out, q).start()

    def ag_copy(d, b, c, slot):
        return pltpu.make_async_remote_copy(
            nrm.at[b, c], nrm.at[b, c], ag_send.at[d, slot], ag_recv.at[b, c],
            device_id={"tp": t + (1 if d == 0 else -1)}, device_id_type=MESH,
        )

    def ag_wait(b, c):
        pltpu.make_async_copy(nrm.at[b, c], nrm.at[b, c], ag_recv.at[b, c]).wait()

    def ag_up(i):
        old = i - 2
        jo = jnp.maximum(old, 0) // C

        @pl.when((old >= 0) & (jo <= t) & (t < n - 1))
        def _():
            ag_copy(0, jo, lax.rem(old, C), lax.rem(i, 2)).wait_send()

        j = jnp.maximum(i, 0) // C
        c = lax.rem(jnp.maximum(i, 0), C)

        @pl.when((i >= 0) & (j < t))
        def _():
            ag_wait(j, c)

        @pl.when((i >= 0) & (j <= t) & (t < n - 1))
        def _():
            ag_copy(0, j, c, lax.rem(i, 2)).start()

    def ag_down(i):
        old = i - 2
        bo = t + jnp.maximum(old, 0) // C

        @pl.when((old >= 0) & (bo < n) & (t > 0))
        def _():
            ag_copy(1, bo, lax.rem(jnp.maximum(old, 0), C), lax.rem(i, 2)).wait_send()

        b = t + i // C
        c = lax.rem(i, C)

        @pl.when((b < n) & (t > 0))
        def _():
            @pl.when(b > t)
            def _():
                ag_wait(b, c)

            ag_copy(1, b, c, lax.rem(i, 2)).start()

    def rs_copy(d, b, c, slot):
        dst = b if d == 0 else jnp.where(b == t - 1, n, b)
        return pltpu.make_async_remote_copy(
            part.at[b, c], part.at[dst, c], rs_send.at[d, slot], rs_recv.at[dst, c],
            device_id={"tp": t + (1 if d == 0 else -1)}, device_id_type=MESH,
        )

    def rs_wait(slot, c):
        pltpu.make_async_copy(part.at[slot, c], part.at[slot, c], rs_recv.at[slot, c]).wait()

    def project(b, c):
        return jnp.dot(att[b], wo[c], preferred_element_type=F32).astype(BF16)

    def rs_step(d, i):
        first = 1 if d == 0 else 0

        def live(b):
            return (b < n) & ((b > t) if d == 0 else (b < t))

        old = i - 2
        bo = first + jnp.maximum(old, 0) // C

        @pl.when((old >= 0) & live(bo))
        def _():
            rs_copy(d, bo, lax.rem(jnp.maximum(old, 0), C), lax.rem(i, 2)).wait_send()

        b = first + jnp.maximum(i, 0) // C
        c = lax.rem(jnp.maximum(i, 0), C)
        has = (t > 0) if d == 0 else (t < n - 1)

        @pl.when((i >= 0) & live(b))
        def _():
            mine = project(b, c)

            @pl.when(has)
            def _():
                rs_wait(b, c)
                part[b, c] = (part[b, c].astype(F32) + mine.astype(F32)).astype(BF16)

            @pl.when(jnp.logical_not(has))
            def _():
                part[b, c] = mine

            rs_copy(d, b, c, lax.rem(i, 2)).start()

    group = QH // KVH
    pieces = kvw // HS
    my_head = (t * heads) // group

    def kv_copy(b, p, k):
        target = lax.rem(t + k, n)
        gid = t * pieces + p
        is_v = gid // KVH
        return target, gid, pltpu.make_async_remote_copy(
            kvown.at[p], kvin.at[b, is_v], kv_send.at[p, k], kv_recv.at[b, is_v],
            device_id={"tp": target}, device_id_type=MESH,
        )

    def compute_block(b):
        if b > 0:
            @pl.when(t == 0)
            def _():
                for c in range(C):
                    ag_wait(b, c)

        if b == 0:
            for cp in wloads:
                cp.wait()
        accq[...] = jnp.zeros_like(accq)
        acckv[...] = jnp.zeros_like(acckv)

        def mm(c, carry):
            x = nrm[b, c]
            acckv[...] += jnp.dot(x, wkv[c], preferred_element_type=F32)
            accq[...] += jnp.dot(x, wq[c], preferred_element_type=F32)
            return carry

        lax.fori_loop(0, C, mm, 0)
        for p in range(pieces):
            kvown[p] = acckv[:, p * HS : (p + 1) * HS].astype(BF16)
        for p in range(pieces):
            gid = t * pieces + p
            for k in range(1, n):
                target, _, cp = kv_copy(b, p, k)

                @pl.when(lax.rem(gid, KVH) == (target * heads) // group)
                def _(cp=cp):
                    cp.start()

            here = lax.rem(gid, KVH) == my_head

            @pl.when(here & (gid < KVH))
            def _(p=p):
                kf[b * rows : (b + 1) * rows, :] = kvown[p]

            @pl.when(here & (gid >= KVH))
            def _(p=p):
                vf[b * rows : (b + 1) * rows, :] = kvown[p]

        for h in range(heads):
            qs[h] = accq[:, h * HS : (h + 1) * HS].astype(BF16)
        for is_v, full in ((0, kf), (1, vf)):
            owner = (is_v * KVH + my_head) // pieces

            @pl.when(owner != t)
            def _(is_v=is_v, full=full):
                pltpu.make_async_copy(kvin.at[b, is_v], kvin.at[b, is_v], kv_recv.at[b, is_v]).wait()
                full[b * rows : (b + 1) * rows, :] = kvin[b, is_v]

        span = (b + 1) * rows
        rowpos = b * rows + lax.broadcasted_iota(jnp.int32, (rows, span), 0)
        colpos = lax.broadcasted_iota(jnp.int32, (rows, span), 1)
        valid = (colpos <= rowpos) & (colpos < length)
        for h in range(heads):
            s = lax.dot_general(
                qs[h], kf[:span, :], (((1,), (1,)), ((), ())), preferred_element_type=F32
            ) * HS ** (-0.5)
            s = jnp.where(valid, s, -1e30)
            e = jnp.exp(s - jnp.max(s, axis=1, keepdims=True))
            pr = (e / jnp.sum(e, axis=1, keepdims=True)).astype(BF16)
            att[b, :, h * HS : (h + 1) * HS] = jnp.dot(
                pr, vf[:span, :], preferred_element_type=F32
            ).astype(BF16)
        for p in range(pieces):
            gid = t * pieces + p
            for k in range(1, n):
                target, _, cp = kv_copy(b, p, k)

                @pl.when(lax.rem(gid, KVH) == (target * heads) // group)
                def _(cp=cp):
                    cp.wait_send()

    skew = (n - 1) * LAG
    marks = [(j + 1) * C + skew for j in range(n - 1)]
    up_end = marks[min(1, n - 2)] + (n - 1) * C + skew + 2
    down_end = marks[0] + (n - 1) * C + skew + 2
    up_base = marks[min(1, n - 2)]

    def ag(k):
        ag_down(k)
        ag_up(k - t * LAG)

    def rs_d(k):
        rs_step(1, k - marks[0] - (n - 1 - t) * LAG)

    def rs_u(k):
        rs_step(0, k - up_base - t * LAG)

    def run(lo, hi, fs):
        def body(k, carry):
            for f in fs:
                f(k)
            return carry

        if hi > lo:
            lax.fori_loop(lo, hi, body, 0)

    run(0, marks[0], [ag])
    for b in range(n):
        compute_block(b)
        if b < steps - 1:
            pol_point(b)
        if b == 0:
            for cp in oloads:
                cp.wait()
        if b < n - 2:
            fs = [ag, rs_d]
            if b >= 1:
                fs.append(rs_u)
            run(marks[b], marks[b + 1], fs)
    for s in range(n, steps - 1):
        pol_point(s)
    top = marks[n - 2]
    run(top, top + 2, [ag, rs_u, rs_d])
    run(top + 2, max(up_end, down_end), [rs_u, rs_d])

    local_last = length - 1 - t * rows
    rowid = lax.broadcasted_iota(jnp.int32, (rows, 1), 0)
    weight = jnp.where(rowid == local_last, 1.0, 0.0) + seq ** (-0.5)

    def fin(c, acc):
        total = project(t, c).astype(F32)

        @pl.when(t > 0)
        def _():
            rs_wait(t, c)

        @pl.when(t < n - 1)
        def _():
            rs_wait(n, c)

        below = jnp.where(t > 0, part[t, c].astype(F32), 0.0)
        above = jnp.where(t < n - 1, part[n, c].astype(F32), 0.0)
        hid = (resid[c].astype(F32) + (total + below + above)).astype(BF16)
        resid[c] = hid
        pltpu.make_async_copy(resid.at[c], chunk_of(out_h.at[0], c), out_sem.at[c]).start()
        return acc + jnp.sum(hid.astype(F32) * head[c].astype(F32), axis=1, keepdims=True)

    score = lax.fori_loop(0, C, fin, jnp.zeros((rows, 1), F32))
    rmy[...] = jnp.broadcast_to(jnp.sum(score * weight, keepdims=True), rmy.shape)
    pol_point(steps - 1)

    def rcopy(k):
        return pltpu.make_async_remote_copy(
            rmy, rin.at[k - 1], r_send.at[k - 1], r_recv.at[k - 1],
            device_id={"tp": lax.rem(t + k, n)}, device_id_type=MESH,
        )

    for k in range(1, n):
        rcopy(k).start()
    total = rmy[...]
    for k in range(1, n):
        rcopy(k).wait()
        total = total + rin[k - 1]
    rew[...] = total
    for c in range(C):
        pltpu.make_async_copy(resid.at[c], chunk_of(out_h.at[0], c), out_sem.at[c]).wait()

    @pl.when(r == 0)
    def _():
        for s in range(steps):
            pol(pol_in, s).wait_send()
        pltpu.make_async_copy(pol_in, pol_out, p_loc).wait()

    for s in range(steps - 1):
        gap = R >> (s + 1)

        @pl.when(lax.rem(r, 2 * gap) == gap)
        def _(s=s):
            for q in range(s + 1, steps):
                pol(pol_out, q).wait_send()


def solution(mesh):
    n, R = mesh.shape["tp"], mesh.shape["rep"]

    def on_device(residual_in, norm_gain, w_query, w_keyval, w_out, score_head, lengths, policy_slots):
        rows, width = residual_in.shape[1:]
        qw, kvw = w_query.shape[1], w_keyval.shape[1]
        heads = qw // HS
        C = CHUNKS
        cols = width // C
        sem = pltpu.SemaphoreType.DMA
        vm = pl.BlockSpec(memory_space=pltpu.VMEM)
        hbm = pl.BlockSpec(memory_space=pl.ANY)
        hidden, reward, policy = pl.pallas_call(
            functools.partial(kernel, n, R, kvw, heads),
            out_shape=(
                jax.ShapeDtypeStruct(residual_in.shape, BF16),
                jax.ShapeDtypeStruct((8, 128), F32),
                jax.ShapeDtypeStruct(policy_slots.shape, BF16),
            ),
            in_specs=[hbm, vm, hbm, hbm, hbm, vm, pl.BlockSpec(memory_space=pltpu.SMEM), hbm],
            out_specs=(hbm, vm, hbm),
            scratch_shapes=[
                pltpu.VMEM((C, cols, qw), BF16),
                pltpu.VMEM((C, cols, kvw), BF16),
                pltpu.VMEM((C, qw, cols), BF16),
                pltpu.VMEM((C, rows, cols), BF16),
                pltpu.VMEM((n, C, rows, cols), BF16),
                pltpu.VMEM((n + 1, C, rows, cols), BF16),
                pltpu.VMEM((heads, rows, HS), BF16),
                pltpu.VMEM((rows, qw), F32),
                pltpu.VMEM((rows, kvw), F32),
                pltpu.VMEM((kvw // HS, rows, HS), BF16),
                pltpu.VMEM((n, 2, rows, HS), BF16),
                pltpu.VMEM((n * rows, HS), BF16),
                pltpu.VMEM((n * rows, HS), BF16),
                pltpu.VMEM((n, rows, qw), BF16),
                pltpu.VMEM((8, 128), F32),
                pltpu.VMEM((n - 1, 8, 128), F32),
                sem((2 * C + 2,)),
                sem((2, 2)),
                sem((n, C)),
                sem((2, 2)),
                sem((n + 1, C)),
                sem((kvw // HS, n)),
                sem((n, 2)),
                sem((n - 1,)),
                sem((n - 1,)),
                sem((R.bit_length() - 1,)),
                sem,
                sem,
                sem((C,)),
            ],
            compiler_params=pltpu.CompilerParams(
                collective_id=0, has_side_effects=True, vmem_limit_bytes=67043328
            ),
        )(
            residual_in,
            norm_gain.reshape(C, 1, cols),
            w_query.reshape(C, cols, qw),
            w_keyval.reshape(C, cols, kvw),
            w_out,
            score_head.reshape(C, 1, cols),
            lengths,
            policy_slots,
        )
        return hidden, reward[0, :1], policy

    return jax.shard_map(
        on_device,
        mesh=mesh,
        in_specs=(
            P("rep", "tp", None),
            P(),
            P(None, "tp"),
            P(None, "tp"),
            P("tp", None),
            P(),
            P("rep"),
            P("rep", None, "tp"),
        ),
        out_specs=(P("rep", "tp", None), P("rep"), P("rep", None, "tp")),
        check_vma=False,
    )
```

time: 397 us -> 337 us (0.85)
  Pallas kernels: 0 us -> 326 us
  waiting for transfers between devices: 304 us -> 0 us
  matrix products: 41.8 us -> 0 us
  other arithmetic: 16.1 us -> 0 us
  between operations: 16.1 us -> 1.3 us
  blocking collectives: 11.7 us -> 0 us
    pallas_call x0 -> x1, Pallas kernels: none -> 326 us  [on_device(): pl.pallas_call(functools.partial(kernel, n, R, kvw, heads), out_shape=(ja...]
    all_gather x2 -> x0, waiting for transfers between devices: 165 us -> none  [the longest x1 152 us: on_device(): piece = lax.all_gather(normed, 'tp', axis=0, tiled=True)]
    reduce_scatter x1 -> x0, waiting for transfers between devices: 139 us -> none  [on_device(): lax.psum_scatter(jnp.dot(attended, w_out, preferred_element_type=jnp.floa...]
    dot_general x19 -> x0, matrix products: 41.8 us -> none  [the longest x1 14.9 us: on_device(): jnp.dot(piece, w_query, preferred_element_type=jnp.float32)]
    psum x1 -> x0, blocking collectives: 11.7 us -> none  [on_device(): reward = lax.psum(contrib, 'tp')]
    reduce_sum x11 -> x0, other arithmetic: 7.92 us -> none  [the longest x1 3.65 us: on_device(): jnp.sum(hidden.astype(jnp.float32) * score_head.astype(jnp.float32)[None,...]
    convert_element_type x3 -> x0, other arithmetic: 4.23 us -> none  [the longest x1 3.5 us: on_device(): (resid * lax.rsqrt(meansq + 1e-05) * norm_gain.astype(jnp.float32)).astyp...]
  transfers between devices with their start and end apart: 4 -> 0, of which waited for: 3 -> 0; matrix products, arithmetic and copies ran while one was open for 6% -> 0% of each run, Pallas kernels for 0% -> 0%
where the time goes in v1:
time: 337 us; the launch traced here: 336 us
  Pallas kernels  326 us (97%)
  local copies, waits for them, and re-layouts  8.78 us (3%)
    pallas_call x1, Pallas kernels, on_device(): pl.pallas_call(functools.partial(kernel, n, R, kvw, heads), out_shape=(ja...  326 us

profile of v1, /device:TPU:0, one launch (start us, length us, event | category | flops | bytes accessed | tf_op | source)
XLA Modules:
  0.0 336.2 jit_solution(4166159787916778455)
XLA Ops:
  1.3 1.3 reshape.22.gain
  2.6 1.3 reshape.23.head
  4.0 326.1 %shard_map.103 = (bf16[1,128,8192]{2,1,0:T(8,128)(2,1)}, f32[8,128]{1,0:T(8,128)}, bf16[1,768,2048]{2,1,0:T(8,128)(2,1)}) custom-call(bf16[1,128,8192]{2,1,0:T(8,128)(2,1)} %resid_h.1, bf16[16,1,512]{2,1,0:T(2,128)(2,1)} %reshape.22.gain, bf16[16,512,1024]{2,1,0:T(8,128)(2,1)} %bitcast.3, bf16[16,512,256]{2,1,0:T(8,128)(2,1)} %bitcast.4, ...), custom_call_target="tpu_custom_call" | custom-call | tf_op jit(solution)/shard_map/pallas_call | solution.py:385
  330.1 0.0 copy-start
  330.1 1.3 slice.3
  331.4 3.1 copy.16
  334.5 0.0 copy-done
  334.5 1.7 copy.17
Async XLA Ops:
  330.1 4.4 %copy-start = (bf16[1,768,2048]{2,1,0:T(8,128)(2,1)S(1)}, bf16[1,768,2048]{2,1,0:T(8,128)(2,1)}, u32[]{:S(2)}) copy-start(bf16[1,768,2048]{2,1,0:T(8,128)(2,1)} %get-tuple-element.14) | copy-start | bytes 9437188

commit v2 on v1

--- a/solution.py
+++ b/solution.py
@@ -13,8 +13,10 @@
 MESH = pl.DeviceIdType.MESH
 F32 = jnp.float32
 BF16 = jnp.bfloat16
-CHUNKS = 16
-LAG = 2
+CHUNKS = 8
+LAG = 3
+DEPTH = 6
+GO = 0
 
 
 def kernel(
@@ -22,7 +24,7 @@
     resid_h, gain, wq_h, wkv_h, wo_h, head, lens, pol_in,
     out_h, rew, pol_out,
     wq, wkv, wo, resid, nrm, part, qs, accq, acckv, kvown, kvin, kf, vf, att, rmy, rin,
-    load_sem, ag_send, ag_recv, rs_send, rs_recv, kv_send, kv_recv, r_send, r_recv, p_send, p_recv, p_loc, out_sem,
+    load_sem, ag_send, ag_recv, rs_send, rs_recv, kv_send, kv_recv, r_send, r_recv, p_send, p_recv, p_loc, out_sem, go_sem,
 ):
     t = lax.axis_index("tp")
     r = lax.axis_index("rep")
@@ -100,12 +102,12 @@
         pltpu.make_async_copy(nrm.at[b, c], nrm.at[b, c], ag_recv.at[b, c]).wait()
 
     def ag_up(i):
-        old = i - 2
+        old = i - DEPTH
         jo = jnp.maximum(old, 0) // C
 
         @pl.when((old >= 0) & (jo <= t) & (t < n - 1))
         def _():
-            ag_copy(0, jo, lax.rem(old, C), lax.rem(i, 2)).wait_send()
+            ag_copy(0, jo, lax.rem(old, C), lax.rem(i, DEPTH)).wait_send()
 
         j = jnp.maximum(i, 0) // C
         c = lax.rem(jnp.maximum(i, 0), C)
@@ -116,15 +118,15 @@
 
         @pl.when((i >= 0) & (j <= t) & (t < n - 1))
         def _():
-            ag_copy(0, j, c, lax.rem(i, 2)).start()
+            ag_copy(0, j, c, lax.rem(i, DEPTH)).start()
 
     def ag_down(i):
-        old = i - 2
+        old = i - DEPTH
         bo = t + jnp.maximum(old, 0) // C
 
         @pl.when((old >= 0) & (bo < n) & (t > 0))
         def _():
-            ag_copy(1, bo, lax.rem(jnp.maximum(old, 0), C), lax.rem(i, 2)).wait_send()
+            ag_copy(1, bo, lax.rem(jnp.maximum(old, 0), C), lax.rem(i, DEPTH)).wait_send()
 
         b = t + i // C
         c = lax.rem(i, C)
@@ -135,7 +137,7 @@
             def _():
                 ag_wait(b, c)
 
-            ag_copy(1, b, c, lax.rem(i, 2)).start()
+            ag_copy(1, b, c, lax.rem(i, DEPTH)).start()
 
     def rs_copy(d, b, c, slot):
         dst = b if d == 0 else jnp.where(b == t - 1, n, b)
@@ -156,12 +158,12 @@
         def live(b):
             return (b < n) & ((b > t) if d == 0 else (b < t))
 
-        old = i - 2
+        old = i - DEPTH
         bo = first + jnp.maximum(old, 0) // C
 
         @pl.when((old >= 0) & live(bo))
         def _():
-            rs_copy(d, bo, lax.rem(jnp.maximum(old, 0), C), lax.rem(i, 2)).wait_send()
+            rs_copy(d, bo, lax.rem(jnp.maximum(old, 0), C), lax.rem(i, DEPTH)).wait_send()
 
         b = first + jnp.maximum(i, 0) // C
         c = lax.rem(jnp.maximum(i, 0), C)
@@ -180,7 +182,7 @@
             def _():
                 part[b, c] = mine
 
-            rs_copy(d, b, c, lax.rem(i, 2)).start()
+            rs_copy(d, b, c, lax.rem(i, DEPTH)).start()
 
     group = QH // KVH
     pieces = kvw // HS
@@ -271,8 +273,8 @@
 
     skew = (n - 1) * LAG
     marks = [(j + 1) * C + skew for j in range(n - 1)]
-    up_end = marks[min(1, n - 2)] + (n - 1) * C + skew + 2
-    down_end = marks[0] + (n - 1) * C + skew + 2
+    up_end = marks[min(1, n - 2)] + (n - 1) * C + skew + DEPTH
+    down_end = marks[0] + (n - 1) * C + skew + DEPTH
     up_base = marks[min(1, n - 2)]
 
     def ag(k):
@@ -294,8 +296,17 @@
         if hi > lo:
             lax.fori_loop(lo, hi, body, 0)
 
+    @pl.when(lax.rem(r, 2) == 1)
+    def _():
+        pl.semaphore_wait(go_sem, 1)
+
     run(0, marks[0], [ag])
     for b in range(n):
+        if b == min(GO, n - 1):
+            @pl.when(lax.rem(r, 2) == 0)
+            def _():
+                pl.semaphore_signal(go_sem, inc=1, device_id={"rep": r + 1}, device_id_type=MESH)
+
         compute_block(b)
         if b < steps - 1:
             pol_point(b)
@@ -310,8 +321,8 @@
     for s in range(n, steps - 1):
         pol_point(s)
     top = marks[n - 2]
-    run(top, top + 2, [ag, rs_u, rs_d])
-    run(top + 2, max(up_end, down_end), [rs_u, rs_d])
+    run(top, top + DEPTH, [ag, rs_u, rs_d])
+    run(top + DEPTH, max(up_end, down_end), [rs_u, rs_d])
 
     local_last = length - 1 - t * rows
     rowid = lax.broadcasted_iota(jnp.int32, (rows, 1), 0)
@@ -409,9 +420,9 @@
                 pltpu.VMEM((8, 128), F32),
                 pltpu.VMEM((n - 1, 8, 128), F32),
                 sem((2 * C + 2,)),
-                sem((2, 2)),
+                sem((2, DEPTH)),
                 sem((n, C)),
-                sem((2, 2)),
+                sem((2, DEPTH)),
                 sem((n + 1, C)),
                 sem((kvw // HS, n)),
                 sem((n, 2)),
@@ -421,6 +432,7 @@
                 sem,
                 sem,
                 sem((C,)),
+                pltpu.SemaphoreType.REGULAR,
             ],
             compiler_params=pltpu.CompilerParams(
                 collective_id=0, has_side_effects=True, vmem_limit_bytes=67043328

time: 337 us -> 301 us (0.89)
  the two profiles are of different devices: /device:TPU:0 before, /device:TPU:1 now
where the time goes in v2:
time: 301 us
  Pallas kernels  291 us (97%)
  local copies, waits for them, and re-layouts  8.78 us (3%)
    pallas_call x1, Pallas kernels, on_device(): pl.pallas_call(functools.partial(kernel, n, R, kvw, heads), out_shape=(ja...  291 us

profile of v2, /device:TPU:1, one launch (start us, length us, event | category | flops | bytes accessed | tf_op | source)
XLA Modules:
  0.0 301.1 jit_solution(16084977646111238378)
XLA Ops:
  1.3 1.3 reshape.22.gain
  2.6 1.3 reshape.23.head
  4.0 291.0 %shard_map.103 = (bf16[1,128,8192]{2,1,0:T(8,128)(2,1)}, f32[8,128]{1,0:T(8,128)}, bf16[1,768,2048]{2,1,0:T(8,128)(2,1)}) custom-call(bf16[1,128,8192]{2,1,0:T(8,128)(2,1)} %resid_h.1, bf16[8,1,1024]{2,1,0:T(2,128)(2,1)} %reshape.22.gain, bf16[8,1024,1024]{2,1,0:T(8,128)(2,1)} %bitcast.3, bf16[8,1024,256]{2,1,0:T(8,128)(2,1)} %bitcast.4, ...), custom_call_target="tpu_custom_call" | custom-call | tf_op jit(solution)/shard_map/pallas_call | solution.py:396
  294.9 0.0 copy-start
  295.0 1.3 slice.3
  296.3 3.1 %copy.16 = bf16[1,128,8192]{2,1,0:T(8,128)(2,1)} copy(bf16[1,128,8192]{2,1,0:T(8,128)(2,1)} %get-tuple-element.12) | data formatting | bytes 4194304
  299.4 0.0 copy-done
  299.4 1.7 copy.17
Async XLA Ops:
  294.9 4.4 %copy-start = (bf16[1,768,2048]{2,1,0:T(8,128)(2,1)S(1)}, bf16[1,768,2048]{2,1,0:T(8,128)(2,1)}, u32[]{:S(2)}) copy-start(bf16[1,768,2048]{2,1,0:T(8,128)(2,1)} %get-tuple-element.14) | copy-start | bytes 9437188
